TPU v7x, 32 devices: a whole 2x2x4 slice. The times are simulated.
32 devices in a mesh: dp: 8 (over y, x, core), tensor: 4 (over z).
Axes of the slice: x: 2, y: 2, z: 4, core: 2. Of those that a mesh axis runs over, the one named last changes fastest.
Arguments:
- inputs: bfloat16 [2048, 2048], P('dp'), may hold values from -6 to 6
- ln_gain: float32 [2048], replicated, may hold values from 0.5 to 1.5
- ln_bias: float32 [2048], replicated, may hold values from -1.75 to 1.75
- w_qkv: bfloat16 [2048, 6144], P(None, 'tensor'), may hold values from -1 to 1
- b_qkv: float32 [6144], P('tensor'), may hold values from -1.75 to 1.75
- w_out: bfloat16 [2048, 2048], P('tensor'), may hold values from -0.75 to 0.75
- b_out: float32 [2048], replicated, may hold values from -1.75 to 1.75
- w_fc1: bfloat16 [2048, 8192], P(None, 'tensor'), may hold values from -0.125 to 0.125
- b_fc1: float32 [8192], P('tensor'), may hold values from -3 to 3
- w_fc2: bfloat16 [8192, 2048], P('tensor'), may hold values from -0.0625 to 0.0625
- b_fc2: float32 [2048], replicated, may hold values from -1.75 to 1.75
- cotangent: bfloat16 [2048, 2048], P('dp')
Outputs:
- output: bfloat16 [2048, 2048], P('dp')
- input_grad: float32 [2048, 2048], P('dp')
- grad_ln_gain: float32 [2048], replicated
- grad_ln_bias: float32 [2048], replicated
- grad_w_qkv: float32 [2048, 6144], P(None, 'tensor')
- grad_b_qkv: float32 [6144], P('tensor')
- grad_w_out: float32 [2048, 2048], P('tensor')
- grad_b_out: float32 [2048], replicated
- grad_w_fc1: float32 [2048, 8192], P(None, 'tensor')
- grad_b_fc1: float32 [8192], P('tensor')
- grad_w_fc2: float32 [8192, 2048], P('tensor')
- grad_b_fc2: float32 [2048], replicated
All inputs are finite; a program needn't handle non-finite values.
Results may differ from a plain program's by a relative error of at most 0.02.
Values may be sent and summed in bfloat16 or wider, within the bound.
A program may use at most 320 MiB of HBM per device.

v0:
```python
import jax
import jax.numpy as jnp
from jax import lax
from jax.sharding import PartitionSpec as P

HD = 64
ROT = 32


EPS = 1e-05
GELU_C = 0.7978845608028654
GELU_A = 0.044715


def gelu(argument):
    inner = GELU_C * (argument + GELU_A * argument * argument * argument)
    return 0.5 * argument * (1.0 + jnp.tanh(inner))


def gelu_slope(argument):
    tangent = jnp.tanh(GELU_C * (argument + GELU_A * argument * argument * argument))
    return 0.5 * (1.0 + tangent) + 0.5 * argument * (1.0 - tangent * tangent) * GELU_C * (
        1.0 + 3.0 * GELU_A * argument * argument
    )


def rotary_tables(length):
    position = jnp.arange(length).astype(jnp.float32)
    freqs = 10000.0 ** (-(jnp.arange(ROT // 2).astype(jnp.float32) * 2.0 / ROT))
    angles = position[:, None] * freqs[None, :]
    return (jnp.cos(angles)[:, None, :], jnp.sin(angles)[:, None, :])


def rotate(tensor, cosine, sine):
    first = tensor[..., : ROT // 2]
    second = tensor[..., ROT // 2 : ROT]
    return jnp.concatenate(
        [first * cosine - second * sine, second * cosine + first * sine, tensor[..., ROT:]], axis=-1
    )


def unrotate(grad, cosine, sine):
    first = grad[..., : ROT // 2]
    second = grad[..., ROT // 2 : ROT]
    return jnp.concatenate(
        [first * cosine + second * sine, second * cosine - first * sine, grad[..., ROT:]], axis=-1
    )


def probabilities(query_rot, key_rot, logsum):
    length = query_rot.shape[0]
    scores = jnp.einsum(
        "qhd,khd->hqk", query_rot, key_rot, preferred_element_type=jnp.float32
    ) * HD ** (-0.5)
    causal = jnp.arange(length)[:, None] >= jnp.arange(length)[None, :]
    scores = jnp.where(causal[None], scores, -1e30)
    top = jnp.max(scores, -1, keepdims=True)
    logsum = top + jnp.log(jnp.sum(jnp.exp(scores - top), -1, keepdims=True))
    return (jnp.exp(scores - logsum), logsum)


def per_device(
    inputs, ln_gain, ln_bias, w_qkv, b_qkv, w_out, b_out, w_fc1, b_fc1, w_fc2, b_fc2, cotangent
):
    length = inputs.shape[0]
    heads = w_out.shape[0] // HD
    cosine, sine = rotary_tables(length)
    widened = inputs.astype(jnp.float32)
    average = jnp.mean(widened, -1, keepdims=True)
    centered = widened - average
    inv_std = lax.rsqrt(jnp.mean(centered * centered, -1, keepdims=True) + EPS)
    normed_hat = centered * inv_std
    normed = (normed_hat * ln_gain + ln_bias).astype(jnp.bfloat16)
    projected = (jnp.dot(normed, w_qkv, preferred_element_type=jnp.float32) + b_qkv).reshape(
        length, heads, 3, HD
    )
    query_rot = rotate(projected[:, :, 0], cosine, sine).astype(jnp.bfloat16)
    key_rot = rotate(projected[:, :, 1], cosine, sine).astype(jnp.bfloat16)
    value_bf = projected[:, :, 2].astype(jnp.bfloat16)
    probs, logsum = probabilities(query_rot, key_rot, None)
    prob_bf = probs.astype(jnp.bfloat16)
    attended = jnp.einsum("hqk,khd->qhd", prob_bf, value_bf, preferred_element_type=jnp.float32)
    attended = attended.astype(jnp.bfloat16).reshape(length, heads * HD)
    hidden_pre = jnp.dot(normed, w_fc1, preferred_element_type=jnp.float32) + b_fc1
    activated = gelu(hidden_pre).astype(jnp.bfloat16)
    partial_value = jnp.dot(attended, w_out, preferred_element_type=jnp.float32) + jnp.dot(
        activated, w_fc2, preferred_element_type=jnp.float32
    )
    total = lax.psum(partial_value, "tensor")
    output = (widened + total + b_out + b_fc2).astype(jnp.bfloat16)
    g_bout = jnp.sum(cotangent.astype(jnp.float32), 0)
    g_w2 = jnp.dot(activated.T, cotangent, preferred_element_type=jnp.float32)
    dhidden = jnp.dot(cotangent, w_fc2.T, preferred_element_type=jnp.float32) * gelu_slope(
        hidden_pre
    )
    g_b1 = jnp.sum(dhidden, 0)
    dhidden_bf = dhidden.astype(jnp.bfloat16)
    g_w1 = jnp.dot(normed.T, dhidden_bf, preferred_element_type=jnp.float32)
    dnormed_local = jnp.dot(dhidden_bf, w_fc1.T, preferred_element_type=jnp.float32)
    g_wout = jnp.dot(attended.T, cotangent, preferred_element_type=jnp.float32)
    dattn_bf = (
        jnp.dot(cotangent, w_out.T, preferred_element_type=jnp.float32)
        .astype(jnp.bfloat16)
        .reshape(length, heads, HD)
    )
    delta = jnp.sum(
        dattn_bf.astype(jnp.float32) * attended.reshape(length, heads, HD).astype(jnp.float32), -1
    )
    dprob = jnp.einsum("qhd,khd->hqk", dattn_bf, value_bf, preferred_element_type=jnp.float32)
    dscore_bf = (probs * (dprob - jnp.transpose(delta)[:, :, None]) * HD ** (-0.5)).astype(
        jnp.bfloat16
    )
    dquery = jnp.einsum("hqk,khd->qhd", dscore_bf, key_rot, preferred_element_type=jnp.float32)
    dkey = jnp.einsum("hqk,qhd->khd", dscore_bf, query_rot, preferred_element_type=jnp.float32)
    dvalue = jnp.einsum("hqk,qhd->khd", prob_bf, dattn_bf, preferred_element_type=jnp.float32)
    dproj = jnp.stack(
        [unrotate(dquery, cosine, sine), unrotate(dkey, cosine, sine), dvalue], axis=2
    ).reshape(length, heads * 3 * HD)
    g_bqkv = jnp.sum(dproj, 0)
    dproj_bf = dproj.astype(jnp.bfloat16)
    g_wqkv = jnp.dot(normed.T, dproj_bf, preferred_element_type=jnp.float32)
    dnormed_local = dnormed_local + jnp.dot(dproj_bf, w_qkv.T, preferred_element_type=jnp.float32)
    dnormed = lax.psum(dnormed_local, "tensor")
    g_gain = jnp.sum(dnormed * normed_hat, 0)
    g_bias = jnp.sum(dnormed, 0)
    scaled = dnormed * ln_gain
    inner = (
        scaled
        - jnp.mean(scaled, -1, keepdims=True)
        - normed_hat * jnp.mean(scaled * normed_hat, -1, keepdims=True)
    )
    input_grad = cotangent.astype(jnp.float32) + inv_std * inner
    g_wqkv, g_bqkv, g_wout, g_bout, g_w1, g_b1, g_w2, g_gain, g_bias = lax.psum(
        (g_wqkv, g_bqkv, g_wout, g_bout, g_w1, g_b1, g_w2, g_gain, g_bias), "dp"
    )
    return (
        output,
        input_grad,
        g_gain,
        g_bias,
        g_wqkv,
        g_bqkv,
        g_wout,
        g_bout,
        g_w1,
        g_b1,
        g_w2,
        g_bout,
    )


def solution(mesh):
    placed = (
        P("dp", None),
        P(),
        P(),
        P(None, "tensor"),
        P("tensor"),
        P("tensor", None),
        P(),
        P(None, "tensor"),
        P("tensor"),
        P("tensor", None),
        P(),
        P("dp", None),
    )
    return jax.shard_map(
        per_device,
        mesh=mesh,
        in_specs=placed,
        out_specs=(
            P("dp", None),
            P("dp", None),
            P(),
            P(),
            P(None, "tensor"),
            P("tensor"),
            P("tensor", None),
            P(),
            P(None, "tensor"),
            P("tensor"),
            P("tensor", None),
            P(),
        ),
        check_vma=False,
    )
```

profile of v0, /device:TPU:0, one launch (start us, length us, event | category | flops | bytes accessed | tf_op | source)
XLA Modules:
  0.0 837.1 jit_solution(13396688774100656092)
XLA Ops:
  7.2 0.0 copy-start
  7.2 0.0 all-reduce.8.cloned.1.call-start
  7.2 0.0 copy-start.3
  7.3 1.6 convert_reduce_fusion
  8.9 1.6 fusion.12
  10.6 0.0 copy-start.2
  10.6 0.0 copy-start.23
  10.6 1.5 convolution_convert_fusion
  12.1 1.1 copy.49
  13.2 5.8 convolution_add_fusion.1
  19.0 3.0 copy.44
  22.0 1.3 fusion.42
  23.3 0.1 copy_bitcast_fusion
  23.5 0.1 multiply_cosine_fusion
  23.6 0.1 subtract_convert_fusion.1
  23.7 0.5 fusion.43
  24.2 0.3 exponential_reduce_fusion
  24.5 0.6 copy-done.6
  25.1 0.5 multiply_reduce_fusion.1
  25.6 0.5 convolution_bitcast_fusion
  26.1 0.0 slice-start.9
  26.1 0.7 multiply_convert_fusion
  26.8 0.4 convolution_bitcast_fusion.1
  27.2 0.0 copy-start.19
  27.2 0.3 convolution_bitcast_fusion.2
  27.5 0.0 slice-start.6
  27.5 0.1 multiply_add_fusion.2
  27.6 1.8 slice-done.9
  29.4 2.5 convolution_add_fusion.3
  32.0 2.6 fusion.36
  34.6 0.0 slice-start.4
  34.6 0.0 slice-start.5
  34.7 3.7 fusion.44
  38.5 0.9 copy-done.10
  39.4 0.1 fusion.23
  39.5 0.1 copy.54
  39.6 0.0 slice-start.11
  39.6 5.0 fusion.45
  44.7 2.1 convolution_add_fusion
  46.8 3.7 convolution_add_fusion.2
  50.5 0.0 all-reduce.8.cloned.1.call-update
  50.5 0.0 all-reduce.6.cloned.1.call-start
  50.6 1.1 copy-done.5
  51.7 0.0 copy-done.14
  51.7 2.7 fusion.46
  54.5 6.9 fusion.38
  61.4 8.7 %fusion.24 = f32[2048,2048]{1,0:T(8,128)} fusion(bf16[256,2048]{1,0:T(8,128)(2,1)S(1)} %copy-done.22, bf16[256,2048]{1,0:T(8,128)(2,1)S(1)} %copy-done.2, f32[2048]{0:T(1024)S(1)} %copy-done.24, f32[2048]{0:T(1024)S(1)} %copy-done.23, f32[256]{0:T(256)S(1)} %add_rsqrt_fusion, f32[256]{0:T(256)S(1)} %broadcast_multiply_fusion.2), kind=kOutput, calls=%fused_computation.54 | convolution fusion | flops 2150629376 | bytes 18892800 | tf_op jit(solution)/shard_map/dot_general | solution.py:98
  70.1 8.8 %fusion.35 = f32[2048,2048]{1,0:T(8,128)} fusion(bf16[256,2048]{1,0:T(8,128)(2,1)S(1)} %copy-done.5, f32[256,2048]{1,0:T(8,128)S(1)} %copy-done.18), kind=kOutput, calls=%fused_computation.83 | convolution fusion | flops 2152202240 | bytes 19922944 | tf_op jit(solution)/shard_map/dot_general | solution.py:92
  78.9 0.0 all-reduce.6.cloned.1.call-update
  79.0 1.0 copy-done.9
  80.0 0.2 copy-done.11
  80.1 1.4 fusion.22
  81.5 0.1 reduce_sum.110
  81.6 126.8 %all-reduce.8.cloned.1.call-done = (f32[256,2048]{1,0:T(8,128)}, f32[256,2048]{1,0:T(8,128)}) async-done(((f32[256,2048]{1,0:T(8,128)}, f32[256,2048]{1,0:T(8,128)}), (f32[256,2048]{1,0:T(8,128)}, f32[256,2048]{1,0:T(8,128)})) %all-reduce.8.cloned.1.call-update) | async-done | bytes 4194320 | tf_op jit(solution)/shard_map/psum | solution.py:89
  208.4 2.7 fusion.11
  211.1 4.8 convert_reduce_fusion.1
  215.9 27.2 %all-reduce = (f32[2048]{0:T(1024)}, f32[2048]{0:T(1024)}, f32[1536]{0:T(1024)}, f32[2048]{0:T(1024)S(1)}, f32[2048]{0:T(1024)}) all-reduce(f32[2048]{0:T(1024)S(1)} %get-tuple-element.12, f32[2048]{0:T(1024)S(1)} %get-tuple-element.15, f32[1536]{0:T(1024)S(1)} %reduce_sum.110, ...), channel_id=1, replica_groups=mesh['dp'=8,'tensor'=4] {'dp'}, use_global_device_ids=true, to_apply=%region_10.11 | all-reduce | flops 9728 | bytes 77824 | tf_op jit(solution)/shard_map/psum | solution.py:133
  243.1 549.5 %all-reduce.6.cloned.1.call-done = (f32[2048,1536]{1,0:T(8,128)}, f32[512,2048]{1,0:T(8,128)}, f32[2048,2048]{1,0:T(8,128)}, f32[2048,2048]{1,0:T(8,128)}) async-done(((f32[2048,1536]{1,0:T(8,128)}, f32[512,2048]{1,0:T(8,128)}, f32[2048,2048]{1,0:T(8,128)}, f32[2048,2048]{1,0:T(8,128)}), (f32[2048,1536]{1,0:T(8,128)}, f32[512,2048]{1,0:T(8,128)}, f32[2048,2048]{1,0:T(8,128)}, ...) | async-done | bytes 50331664 | tf_op jit(solution)/shard_map/psum | solution.py:133
  792.6 0.6 copy.80
  793.2 10.6 %copy.81 = f32[2048,1536]{1,0:T(8,128)} copy(f32[2048,1536]{1,0:T(8,128)} %get-tuple-element.84) | data formatting | bytes 25165824
  803.8 4.8 copy.82
  808.7 13.6 %copy.83 = f32[2048,2048]{1,0:T(8,128)} copy(f32[2048,2048]{1,0:T(8,128)} %get-tuple-element.88) | data formatting | bytes 33554432
  822.2 1.7 slice-done.3
  824.0 6.3 copy.84
  (83 shorter events, 0.3 us)
Async XLA Ops:
  7.2 3.4 copy-start
  7.2 201.2 %all-reduce.8.cloned.1.call-start = ((), (), s32[]{:S(2)}) async-start(), calls=%async_computation.1 | async-start | bytes 8388608 | tf_op jit(solution)/shard_map/psum | solution.py:89
  7.2 3.3 copy-start.3
  10.6 2.6 copy-start.2
  10.6 2.6 copy-start.23
  10.6 2.6 copy-start.24
  10.6 2.6 copy-start.28
  23.7 1.4 copy-start.6
  25.1 2.5 slice-start.8
  25.6 19.1 %copy-start.13 = (bf16[8,64,256]{2,1,0:T(8,128)(2,1)}, bf16[8,64,256]{2,1,0:T(8,128)(2,1)S(1)}, u32[]{:S(2)}) copy-start(bf16[8,64,256]{2,1,0:T(8,128)(2,1)S(1)} %get-tuple-element.49) | copy-start | bytes 786436
  26.1 12.4 %copy-start.12 = (f32[256,8,1,64]{0,3,1,2:T(8,128)}, f32[256,8,1,64]{0,3,1,2:T(8,128)S(1)}, u32[]{:S(2)}) copy-start(f32[256,8,1,64]{0,3,1,2:T(8,128)S(1)} %convolution_bitcast_fusion) | copy-start | bytes 1572868
  26.1 3.3 slice-start.9
  27.2 4.7 copy-start.19
  27.2 2.2 copy-start.29
  27.5 4.4 copy-start.20
  27.5 4.4 slice-start.6
  29.4 2.5 slice-start.7
  32.0 2.7 copy-start.17
  32.0 2.7 copy-start.4
  34.6 3.7 slice-start.4
  34.6 3.8 slice-start.5
  38.3 8.5 %copy-start.21 = (bf16[256,2048]{1,0:T(8,128)(2,1)}, bf16[256,2048]{1,0:T(8,128)(2,1)S(1)}, u32[]{:S(2)}) copy-start(bf16[256,2048]{1,0:T(8,128)(2,1)S(1)} %get-tuple-element.51) | copy-start | bytes 3145732
  38.4 1.2 copy-start.8
  38.5 0.9 copy-start.10
  39.4 7.4 slice-start.10
  39.6 5.1 copy-start.15
  39.6 7.2 slice-start.11
  50.5 1.2 copy-start.5
  50.5 1.3 copy-start.14
  50.5 4.0 copy-start.16
  50.5 742.1 %all-reduce.6.cloned.1.call-start = ((), (), s32[]{:S(2)}) async-start(), calls=%async_computation | async-start | bytes 100663296 | tf_op jit(solution)/shard_map/psum | solution.py:133
  54.5 6.9 copy-start.22
  61.4 8.7 %copy-start.18 = (f32[256,2048]{1,0:T(8,128)S(1)}, f32[256,2048]{1,0:T(8,128)}, u32[]{:S(2)}) copy-start(f32[256,2048]{1,0:T(8,128)} %copy-done.17) | copy-start | bytes 6291460
  78.9 1.0 copy-start.9
  78.9 1.2 copy-start.11
  80.1 131.0 %copy-start.26 = (f32[2048]{0:T(1024)S(1)}, f32[2048]{0:T(1024)}, u32[]{:S(2)}) copy-start(f32[2048]{0:T(1024)} %param.22) | copy-start | bytes 24580
  80.1 131.0 %copy-start.27 = (f32[2048]{0:T(1024)S(1)}, f32[2048]{0:T(1024)}, u32[]{:S(2)}) copy-start(f32[2048]{0:T(1024)} %param.18) | copy-start | bytes 24580
  208.4 2.7 copy-start.7
  243.1 560.7 %copy-start.25 = (f32[2048]{0:T(1024)}, f32[2048]{0:T(1024)S(1)}, u32[]{:S(2)}) copy-start(f32[2048]{0:T(1024)S(1)} %get-tuple-element.87) | copy-start | bytes 24580
  803.8 18.4 %slice-start = ((s8[16777216]{0:T(1024)(128)(4,1)}), s8[4194304]{0:T(1024)(128)(4,1)S(1)}, s32[]{:S(2)}) async-start(s8[16777216]{0:T(1024)(128)(4,1)} %bitcast.53), calls=%async_computation.2 | async-start | bytes 8388608
  808.7 13.6 %slice-start.1 = ((s8[16777216]{0:T(1024)(128)(4,1)}), s8[4194304]{0:T(1024)(128)(4,1)S(1)}, s32[]{:S(2)}) async-start(s8[16777216]{0:T(1024)(128)(4,1)} %bitcast.53), calls=%async_computation.3 | async-start | bytes 8388608
  808.7 13.6 %slice-start.2 = ((s8[16777216]{0:T(1024)(128)(4,1)}), s8[4194304]{0:T(1024)(128)(4,1)S(1)}, s32[]{:S(2)}) async-start(s8[16777216]{0:T(1024)(128)(4,1)} %bitcast.53), calls=%async_computation.4 | async-start | bytes 8388608
  808.7 15.3 %slice-start.3 = ((s8[16777216]{0:T(1024)(128)(4,1)}), s8[4194304]{0:T(1024)(128)(4,1)S(1)}, s32[]{:S(2)}) async-start(s8[16777216]{0:T(1024)(128)(4,1)} %bitcast.53), calls=%async_computation.5 | async-start | bytes 8388608
  824.0 6.3 copy-start.1
Sparse Core Ops, SparseCore 0:
  50.6 157.7 all-reduce.7
  213.8 578.7 all-reduce.5
where the time goes:
time: 838 us; the launch traced here: 837 us
  waiting for transfers between devices  676 us (81%)
  matrix products  56.8 us (7%)
  local copies, waits for them, and re-layouts  49.1 us (6%)
  blocking collectives  27.2 us (3%)
  between operations  14.7 us (2%)
  other arithmetic  13 us (2%)
    psum x1, waiting for transfers between devices, per_device(): lax.psum((g_wqkv, g_bqkv, g_wout, g_bout, g_w1, g_b1, g_w2, g_gain, g_bia...  549 us
    psum x1, waiting for transfers between devices, per_device(): total = lax.psum(partial_value, 'tensor')  127 us
    unnamed x85, local copies, waits for them, and re-layouts  43.4 us
    psum x1, blocking collectives, per_device(): lax.psum((g_wqkv, g_bqkv, g_wout, g_bout, g_w1, g_b1, g_w2, g_gain, g_bia...  27.2 us
  transfers between devices with their start and end apart: 2, of which 2 were waited for; matrix products, arithmetic and copies ran while one was open for 4% of the time, Pallas kernels for 0%

commit v1 on v0

v1 whole, which is shorter than its diff:
```python
import jax
import jax.numpy as jnp
from jax import lax
from jax.sharding import PartitionSpec as P

HD = 64
ROT = 32
EPS = 1e-05
GELU_C = 0.7978845608028654
GELU_A = 0.044715
BF = jnp.bfloat16
F32 = jnp.float32


def gelu_pair(u):
    tangent = jnp.tanh(GELU_C * (u + GELU_A * u * u * u))
    act = 0.5 * u * (1.0 + tangent)
    slope = 0.5 * (1.0 + tangent) + 0.5 * u * (1.0 - tangent * tangent) * GELU_C * (
        1.0 + 3.0 * GELU_A * u * u
    )
    return act, slope


def rotary_tables(length):
    position = jnp.arange(length).astype(F32)
    freqs = 10000.0 ** (-(jnp.arange(ROT // 2).astype(F32) * 2.0 / ROT))
    angles = position[:, None] * freqs[None, :]
    return (jnp.cos(angles)[:, None, :], jnp.sin(angles)[:, None, :])


def rotate(tensor, cosine, sine):
    first = tensor[..., : ROT // 2]
    second = tensor[..., ROT // 2 : ROT]
    return jnp.concatenate(
        [first * cosine - second * sine, second * cosine + first * sine, tensor[..., ROT:]], axis=-1
    )


def dot(a, b):
    return jnp.dot(a, b, preferred_element_type=F32)


def dot_nt(a, b):
    return lax.dot_general(a, b, (((1,), (1,)), ((), ())), preferred_element_type=F32)


def dot_tn(a, b):
    return lax.dot_general(a, b, (((0,), (0,)), ((), ())), preferred_element_type=F32)


def layer_norm(x, ln_gain, ln_bias):
    widened = x.astype(F32)
    average = jnp.mean(widened, -1, keepdims=True)
    centered = widened - average
    inv_std = lax.rsqrt(jnp.mean(centered * centered, -1, keepdims=True) + EPS)
    xhat = centered * inv_std
    return (xhat * ln_gain + ln_bias).astype(BF), xhat, inv_std


def attention(proj, dattn, length):
    rows = proj.shape[0]
    seqs = rows // length
    heads = dattn.shape[1] // HD
    cosine, sine = rotary_tables(length)
    projected = proj.reshape(seqs, length, heads, 3, HD)
    query = rotate(projected[:, :, :, 0], cosine, sine).astype(BF)
    key = rotate(projected[:, :, :, 1], cosine, sine).astype(BF)
    value = projected[:, :, :, 2].astype(BF)
    dattn = dattn.astype(BF).reshape(seqs, length, heads, HD)
    scores = jnp.einsum("sqhd,skhd->shqk", query, key, preferred_element_type=F32) * HD ** (-0.5)
    causal = jnp.arange(length)[:, None] >= jnp.arange(length)[None, :]
    scores = jnp.where(causal, scores, -1e30)
    top = jnp.max(scores, -1, keepdims=True)
    expo = jnp.exp(scores - top)
    probs = expo / jnp.sum(expo, -1, keepdims=True)
    prob_bf = probs.astype(BF)
    attended = jnp.einsum("shqk,skhd->sqhd", prob_bf, value, preferred_element_type=F32).astype(BF)
    delta = jnp.sum(dattn.astype(F32) * attended.astype(F32), -1)
    dprob = jnp.einsum("sqhd,skhd->shqk", dattn, value, preferred_element_type=F32)
    dscore = (probs * (dprob - jnp.swapaxes(delta, 1, 2)[..., None]) * HD ** (-0.5)).astype(BF)
    dquery = jnp.einsum("shqk,skhd->sqhd", dscore, key, preferred_element_type=F32)
    dkey = jnp.einsum("shqk,sqhd->skhd", dscore, query, preferred_element_type=F32)
    dvalue = jnp.einsum("shqk,sqhd->skhd", prob_bf, dattn, preferred_element_type=F32)
    dproj = jnp.stack(
        [rotate(dquery, cosine, -sine), rotate(dkey, cosine, -sine), dvalue], axis=3
    ).reshape(rows, heads * 3 * HD)
    return attended.reshape(rows, heads * HD), dproj.astype(BF), jnp.sum(dproj, 0)


def per_device(
    inputs, ln_gain, ln_bias, w_qkv, b_qkv, w_out, b_out, w_fc1, b_fc1, w_fc2, b_fc2, cotangent
):
    length = inputs.shape[0]
    n_dp = lax.axis_size("dp")
    n_tp = lax.axis_size("tensor")
    chips = n_dp // 2
    bits = chips.bit_length() - 1
    core = lax.axis_index("dp") % 2

    def hop(array, bit):
        perm = [(i, i ^ (2 << (bit if i % 2 == 0 else bits - 1 - bit))) for i in range(n_dp)]
        return lax.ppermute(array, "dp", perm)

    def sibling(array):
        return lax.ppermute(array, "dp", [(i, i ^ 1) for i in range(n_dp)])

    def half(array, axis):
        size = array.shape[axis] // 2
        return lax.dynamic_slice_in_dim(array, core * size, size, axis)

    def gather(array):
        got = {0: array}
        for mask in range(1, chips):
            low = (mask & -mask).bit_length() - 1
            got[mask] = hop(got[mask & (mask - 1)], low)
        return [jnp.concatenate([got[m], sibling(got[m])]) for m in range(chips)]

    xs = gather(inputs)
    gs = gather(cotangent)
    wq, bq = half(w_qkv, 1), half(b_qkv, 0)
    wo = half(w_out, 0)
    w1, b1 = half(w_fc1, 1), half(b_fc1, 0)
    w2 = half(w_fc2, 0)

    normed_all, act_all, dhid_all, att_all, dproj_all = [], [], [], [], []
    g_b1 = g_bqkv = 0.0
    for m in range(chips):
        x, g = xs[m], gs[m]
        normed, xhat, inv_std = layer_norm(x, ln_gain, ln_bias)
        hpre = dot(normed, w1) + b1
        act, slope = gelu_pair(hpre)
        act = act.astype(BF)
        dhid = dot_nt(g, w2) * slope
        g_b1 = g_b1 + jnp.sum(dhid, 0)
        dhid = dhid.astype(BF)
        att, dproj, gb = attention(dot(normed, wq) + bq, dot_nt(g, wo), length)
        g_bqkv = g_bqkv + gb
        if m == 0:
            part_out = dot(att, wo) + dot(act, w2)
            part_dn = dot_nt(dhid, w1) + dot_nt(dproj, wq)
            xhat_own, inv_own = xhat[:length], inv_std[:length]
        normed_all.append(normed)
        act_all.append(act)
        dhid_all.append(dhid)
        att_all.append(att)
        dproj_all.append(dproj)

    def reduce_tensor(part):
        own = part[:length] + sibling(part[length:].astype(BF)).astype(F32)
        own = own.astype(BF)
        index = lax.axis_index("tensor")
        steps = n_tp.bit_length() - 1
        held = own
        for s in range(steps):
            rows = held.shape[0] // 2
            bit = (index >> s) & 1
            keep = jnp.where(bit == 0, held[:rows], held[rows:])
            send = jnp.where(bit == 0, held[rows:], held[:rows])
            came = lax.ppermute(send, "tensor", [(i, i ^ (1 << s)) for i in range(n_tp)])
            held = (keep.astype(F32) + came.astype(F32)).astype(BF)
        for s in reversed(range(steps)):
            bit = (index >> s) & 1
            came = lax.ppermute(held, "tensor", [(i, i ^ (1 << s)) for i in range(n_tp)])
            held = jnp.where(
                bit == 0, jnp.concatenate([held, came]), jnp.concatenate([came, held])
            )
        return held.astype(F32)

    total = reduce_tensor(part_out)
    output = (inputs.astype(F32) + total + b_out + b_fc2).astype(BF)
    dnormed = reduce_tensor(part_dn)
    norms = jnp.stack([jnp.sum(dnormed * xhat_own, 0), jnp.sum(dnormed, 0)])
    scaled = dnormed * ln_gain
    inner = (
        scaled
        - jnp.mean(scaled, -1, keepdims=True)
        - xhat_own * jnp.mean(scaled * xhat_own, -1, keepdims=True)
    )
    input_grad = cotangent.astype(F32) + inv_own * inner
    for bit in range(bits + 1):
        norms = norms + lax.ppermute(norms, "dp", [(i, i ^ (1 << bit)) for i in range(n_dp)])

    normed_all = jnp.concatenate(normed_all)
    g_all = jnp.concatenate(gs)
    g_bout = jnp.sum(g_all.astype(F32), 0)

    def both_halves(own, axis):
        own = own.astype(BF)
        came = sibling(own)
        return jnp.where(
            core == 0,
            jnp.concatenate([own, came], axis),
            jnp.concatenate([came, own], axis),
        ).astype(F32)

    def both_bias(own):
        came = sibling(own)
        return jnp.where(core == 0, jnp.concatenate([own, came]), jnp.concatenate([came, own]))

    g_w2 = both_halves(dot_tn(jnp.concatenate(act_all), g_all), 0)
    g_w1 = both_halves(dot_tn(normed_all, jnp.concatenate(dhid_all)), 1)
    g_wout = both_halves(dot_tn(jnp.concatenate(att_all), g_all), 0)
    g_wqkv = both_halves(dot_tn(normed_all, jnp.concatenate(dproj_all)), 1)
    return (
        output,
        input_grad,
        norms[0],
        norms[1],
        g_wqkv,
        both_bias(g_bqkv),
        g_wout,
        g_bout,
        g_w1,
        both_bias(g_b1),
        g_w2,
        g_bout,
    )


def solution(mesh):
    placed = (
        P("dp", None),
        P(),
        P(),
        P(None, "tensor"),
        P("tensor"),
        P("tensor", None),
        P(),
        P(None, "tensor"),
        P("tensor"),
        P("tensor", None),
        P(),
        P("dp", None),
    )
    return jax.shard_map(
        per_device,
        mesh=mesh,
        in_specs=placed,
        out_specs=(
            P("dp", None),
            P("dp", None),
            P(),
            P(),
            P(None, "tensor"),
            P("tensor"),
            P("tensor", None),
            P(),
            P(None, "tensor"),
            P("tensor"),
            P("tensor", None),
            P(),
        ),
        check_vma=False,
    )
```

time: 838 us -> 547 us (0.65)
  waiting for transfers between devices: 676 us -> 105 us
  local copies, waits for them, and re-layouts: 49.1 us -> 160 us
  matrix products: 56.8 us -> 154 us
  other arithmetic: 13 us -> 93.4 us
  blocking collectives: 27.2 us -> 0 us
  starting transfers between devices: 0.08 us -> 24.2 us
  between operations: 14.7 us -> 2.5 us
    psum x2 -> x0, waiting for transfers between devices: 676 us -> none  [the longest x1 549 us: per_device(): lax.psum((g_wqkv, g_bqkv, g_wout, g_bout, g_w1, g_b1, g_w2, g_gain, g_bia...]
    ppermute x0 -> x33, waiting for transfers between devices: none -> 105 us  [the longest x4 43.3 us: reduce_tensor(): came = lax.ppermute(send, 'tensor', [(i, i ^ 1 << s) for i in range(n_tp)])]
    dot_general x18 -> x44, matrix products: 56.8 us -> 140 us  [the longest x4 43 us: dot_tn(): lax.dot_general(a, b, (((0,), (0,)), ((), ())), preferred_element_type=F32)]
    convert_element_type x2 -> x21, other arithmetic: 0.14 us -> 55.4 us  [the longest x4 39.8 us: both_halves(): return jnp.where(core == 0, jnp.concatenate([own, came], axis), jnp.conca...]
    unnamed x85 -> x275, local copies, waits for them, and re-layouts: 43.4 us -> 83.5 us
    psum x1 -> x0, blocking collectives: 27.2 us -> none  [per_device(): lax.psum((g_wqkv, g_bqkv, g_wout, g_bout, g_w1, g_b1, g_w2, g_gain, g_bia...]
    ppermute x0 -> x33, starting transfers between devices: none -> 24.2 us  [the longest x6 9.46 us: hop(): return lax.ppermute(array, 'dp', perm)]
    reshape x0 -> x12, local copies, waits for them, and re-layouts: none -> 23.3 us  [the longest x4 12.5 us: attention(): projected = proj.reshape(seqs, length, heads, 3, HD)]
  transfers between devices with their start and end apart: 2 -> 33, of which waited for: 2 -> 11; matrix products, arithmetic and copies ran while one was open for 4% -> 59% of each run, Pallas kernels for 0% -> 0%
where the time goes in v1:
time: 547 us; the launch traced here: 539 us
  local copies, waits for them, and re-layouts  160 us (29%)
  matrix products  154 us (28%)
  waiting for transfers between devices  105 us (19%)
  other arithmetic  93.4 us (17%)
  starting transfers between devices  24.2 us (4%)
    unnamed x275, local copies, waits for them, and re-layouts  83.5 us
    ppermute x4, waiting for transfers between devices, reduce_tensor(): came = lax.ppermute(send, 'tensor', [(i, i ^ 1 << s) for i in range(n_tp)])  43.3 us
    dot_general x4, matrix products, dot_tn(): lax.dot_general(a, b, (((0,), (0,)), ((), ())), preferred_element_type=F32)  43 us
    dot_general x10, matrix products, dot(): return jnp.dot(a, b, preferred_element_type=F32)  42.7 us
    convert_element_type x4, other arithmetic, both_halves(): return jnp.where(core == 0, jnp.concatenate([own, came], axis), jnp.conca...  39.8 us
    dot_general x10, matrix products, dot_nt(): lax.dot_general(a, b, (((1,), (1,)), ((), ())), preferred_element_type=F32)  36.5 us
    ppermute x4, waiting for transfers between devices, reduce_tensor(): came = lax.ppermute(held, 'tensor', [(i, i ^ 1 << s) for i in range(n_tp)])  34.3 us
    ppermute x6, waiting for transfers between devices, hop(): return lax.ppermute(array, 'dp', perm)  26.2 us
  transfers between devices with their start and end apart: 33, of which 11 were waited for; matrix products, arithmetic and copies ran while one was open for 59% of the time, Pallas kernels for 0%

profile of v1, /device:TPU:0, one launch (start us, length us, event | category | flops | bytes accessed | tf_op | source)
XLA Modules:
  0.0 539.5 jit_solution(13693362112698537902)
XLA Ops:
  1.2 2.6 collective-permute-start.17
  9.4 2.3 constant_dynamic-update-slice_fusion.15
  18.8 11.5 %collective-permute-done.15 = bf16[256,2048]{1,0:T(8,128)(2,1)} collective-permute-done((bf16[256,2048]{1,0:T(8,128)(2,1)}, bf16[256,2048]{1,0:T(8,128)(2,1)}, u32[]{:S(2)}, u32[]{:S(2)}) %collective-permute-start.15) | collective-permute-done | bytes 1048608 | tf_op jit(solution)/shard_map/ppermute | solution.py:102
  35.6 14.7 %collective-permute-done.21 = bf16[256,2048]{1,0:T(8,128)(2,1)} collective-permute-done((bf16[256,2048]{1,0:T(8,128)(2,1)}, bf16[256,2048]{1,0:T(8,128)(2,1)}, u32[]{:S(2)}, u32[]{:S(2)}) %collective-permute-start.21) | collective-permute-done | bytes 1048608 | tf_op jit(solution)/shard_map/ppermute | solution.py:102
  50.8 2.8 constant_dynamic-update-slice_fusion.13
  60.7 2.1 fusion.19
  62.8 8.0 %fusion.7 = (f32[512,2048]{1,0:T(8,128)}, bf16[512,2048]{1,0:T(8,128)(2,1)S(1)}, bf16[512,2048]{1,0:T(8,128)(2,1)}, bf16[512,2048]{1,0:T(8,128)(2,1)}) fusion(f32[512]{0:T(512)S(1)} %add_rsqrt_fusion.3, f32[512]{0:T(512)S(1)} %broadcast_multiply_fusion.3, bf16[256,2048]{1,0:T(8,128)(2,1)} %collective-permute-done, bf16[256,2048]{1,0:T(8,128)(2,1)S(1)} %copy-done.3, ...), kind=kLoop, calls=%fused_computation.20 | loop fusion | flops 28311552 | bytes 16805888 | tf_op jit(solution)/shard_map/mul | solution.py:56
  72.1 2.9 fusion.133
  75.1 3.1 copy.133
  78.1 3.1 reshape.260
  81.2 5.5 %fusion.136 = f32[512,768]{1,0:T(8,128)} fusion(bf16[512,2048]{1,0:T(8,128)(2,1)} %get-tuple-element.143, bf16[2048,1536]{1,0:T(8,128)(2,1)} %param.15, s32[]{:T(128)S(6)} %select_n.143, f32[768]{0:T(1024)S(1)} %dynamic_slice.19), kind=kOutput, calls=%fused_computation.181 | convolution fusion | flops 1611005952 | bytes 6818820 | tf_op jit(solution)/shard_map/dot_general | solution.py:40
  86.6 3.1 copy.148
  89.7 3.0 reshape.263
  92.8 5.5 %fusion.139 = f32[512,768]{1,0:T(8,128)} fusion(bf16[512,2048]{1,0:T(8,128)(2,1)} %get-tuple-element.144, bf16[2048,1536]{1,0:T(8,128)(2,1)} %param.15, s32[]{:T(128)S(6)} %select_n.143, f32[768]{0:T(1024)S(1)} %dynamic_slice.19), kind=kOutput, calls=%fused_computation.182 | convolution fusion | flops 1611005952 | bytes 6818820 | tf_op jit(solution)/shard_map/dot_general | solution.py:40
  98.2 3.1 copy.162
  101.3 3.2 reshape.265
  105.9 2.7 fusion.243
  111.2 2.4 constant_dynamic-update-slice_fusion.12
  121.3 3.1 fusion.249
  130.6 4.7 fusion.78
  135.7 3.3 constant_dynamic-update-slice_fusion.11
  139.1 4.1 fusion.240
  143.2 4.9 fusion.76
  148.0 2.4 constant_dynamic-update-slice_fusion.10
  152.9 3.7 fusion.72
  165.9 2.0 reshape.274
  173.9 3.0 constant_dynamic-update-slice_fusion.9
  176.9 7.4 %fusion.241 = (f32[1024]{0:T(1024)}, bf16[512,1024]{1,0:T(8,128)(2,1)}) fusion(f32[512,1024]{1,0:T(8,128)S(1)} %copy-done.110, f32[1024]{0:T(1024)S(1)} %copy-done.104, bf16[512,2048]{1,0:T(8,128)(2,1)S(1)} %copy-done.68, bf16[2048,2048]{1,0:T(8,128)(2,1)} %param.21, s32[]{:T(128)S(6)} %select_n.146), kind=kOutput, calls=%fused_computation.412 | convolution fusion | flops 2158492672 | bytes 9445380 | tf_op jit(solution)/shard_map/dot_general | solution.py:44
  187.8 2.1 fusion.18
  191.2 3.0 fusion.142
  194.2 3.0 copy.176
  197.2 3.2 reshape.267
  203.2 3.9 fusion.248
  217.7 3.7 fusion.250
  227.7 6.0 %fusion.70 = f32[512,1024]{1,0:T(8,128)} fusion(bf16[512,2048]{1,0:T(8,128)(2,1)S(1)} %copy-done.26, bf16[2048,2048]{1,0:T(8,128)(2,1)} %param.19, s32[]{:T(128)S(6)} %select_n.146), kind=kOutput, calls=%fused_computation.95 | convolution fusion | flops 2147483648 | bytes 8388612 | tf_op jit(solution)/shard_map/dot_general | solution.py:40
  233.7 2.4 constant_dynamic-update-slice_fusion.8
  238.9 2.0 reshape.275
  242.9 3.8 fusion.251
  261.8 6.0 %multiply_convert_fusion.2 = (bf16[512,1024]{1,0:T(8,128)(2,1)}, bf16[512,1024]{1,0:T(8,128)(2,1)}, bf16[512,1024]{1,0:T(8,128)(2,1)}, bf16[512,1024]{1,0:T(8,128)(2,1)S(1)}, f32[512,1024]{1,0:T(8,128)}) fusion(f32[1024]{0:T(1024)S(1)} %copy-done.105, f32[512,1024]{1,0:T(8,128)S(1)} %copy-done.112, f32[512,1024]{1,0:T(8,128)S(1)} %copy-done.111, ...), kind=kOutput, calls=%fused_computation.148 | convolution fusion | flops 2168455168 | bytes 18878468 | tf_op jit(solution)/shard_map/dot_general | solution.py:40
  267.8 7.1 %fusion.242 = (f32[1024]{0:T(1024)S(1)}, bf16[512,1024]{1,0:T(8,128)(2,1)}) fusion(f32[512,1024]{1,0:T(8,128)S(1)} %copy-done.112, f32[1024]{0:T(1024)S(1)} %copy-done.105, bf16[512,2048]{1,0:T(8,128)(2,1)S(1)} %copy-done.63, bf16[2048,2048]{1,0:T(8,128)(2,1)} %param.21, s32[]{:T(128)S(6)} %select_n.146), kind=kOutput, calls=%fused_computation.413 | convolution fusion | flops 2158492672 | bytes 9445380 | tf_op jit(solution)/shard_map/dot_general | solution.py:44
  274.9 4.7 fusion.68
  292.4 8.4 %convolution_convert_fusion = bf16[2048,768]{0,1:T(8,128)(2,1)} fusion(bf16[512,768]{0,1:T(8,128)(2,1)S(1)} %bitcast.216, bf16[512,768]{0,1:T(8,128)(2,1)S(1)} %bitcast.217, bf16[512,768]{0,1:T(8,128)(2,1)S(1)} %bitcast.218, bf16[512,768]{0,1:T(8,128)(2,1)S(1)} %bitcast.199, bf16[512,2048]{1,0:T(8,128)(2,1)S(1)} %copy-done.27, ...), kind=kOutput, calls=%fused_computation.60 | convolution fusion | flops 6490161152 | bytes 14680064 | tf_op jit(solution)/shard_map/dot_general | solution.py:48
  302.1 5.9 %convolution_convert_fusion.1 = bf16[256,2048]{1,0:T(8,128)(2,1)S(1)} fusion(bf16[2048,2048]{1,0:T(8,128)(2,1)} %get-tuple-element.69, bf16[512,256]{0,1:T(8,128)(2,1)S(1)} %bitcast.220, bf16[512,256]{0,1:T(8,128)(2,1)S(1)} %bitcast.221, bf16[512,256]{0,1:T(8,128)(2,1)S(1)} %bitcast.219, bf16[512,256]{0,1:T(8,128)(2,1)S(1)} %bitcast.211), kind=kOutput, calls=%fused_computation.84 | convolution fusion | flops 2152202240 | bytes 10485760 | tf_op jit(solution)/shard_map/dot_general | solution.py:48
  308.2 6.8 %fusion.239 = (f32[1024]{0:T(1024)S(1)}, bf16[512,1024]{1,0:T(8,128)(2,1)}) fusion(f32[512,1024]{1,0:T(8,128)S(1)} %copy-done.113, f32[1024]{0:T(1024)S(1)} %copy-done.105, bf16[512,2048]{1,0:T(8,128)(2,1)S(1)} %copy-done.66, bf16[2048,2048]{1,0:T(8,128)(2,1)} %param.21, s32[]{:T(128)S(6)} %select_n.146), kind=kOutput, calls=%fused_computation.410 | convolution fusion | flops 2158492672 | bytes 9445380 | tf_op jit(solution)/shard_map/dot_general | solution.py:44
  315.0 13.9 %fusion.44 = bf16[2048,1024]{0,1:T(8,128)(2,1)} fusion(bf16[512,1024]{1,0:T(8,128)(2,1)} %get-tuple-element.60, bf16[512,1024]{1,0:T(8,128)(2,1)} %get-tuple-element.58, bf16[512,1024]{1,0:T(8,128)(2,1)} %get-tuple-element.54, bf16[512,1024]{1,0:T(8,128)(2,1)} %copy-done.114, bf16[512,2048]{1,0:T(8,128)(2,1)} %copy-done.25, ...), kind=kOutput, calls=%fused_computation.58 | convolution fusion | flops 8642363392 | bytes 16777216 | tf_op jit(solution)/shard_map/dot_general | solution.py:48
  328.9 14.8 %fusion.47 = bf16[1024,2048]{0,1:T(8,128)(2,1)} fusion(bf16[2048,2048]{1,0:T(8,128)(2,1)} %get-tuple-element.69, bf16[512,1024]{1,0:T(8,128)(2,1)} %get-tuple-element.148, bf16[512,1024]{1,0:T(8,128)(2,1)} %get-tuple-element.149, bf16[512,1024]{1,0:T(8,128)(2,1)} %get-tuple-element.147, bf16[512,1024]{1,0:T(8,128)(2,1)} %copy-done.115), kind=kOutput, calls=%fused_computation.59 | convolution fusion | flops 8608808960 | bytes 16777216 | tf_op jit(solution)/shard_map/dot_general | solution.py:48
  343.8 4.9 convert_reduce_fusion
  355.0 11.0 %collective-permute-done.8 = bf16[128,2048]{1,0:T(8,128)(2,1)S(1)} collective-permute-done((bf16[128,2048]{1,0:T(8,128)(2,1)S(1)}, bf16[128,2048]{1,0:T(8,128)(2,1)S(1)}, u32[]{:S(2)}, u32[]{:S(2)}) %collective-permute-start.8) | collective-permute-done | bytes 524320 | tf_op jit(solution)/shard_map/ppermute | solution.py:159
  367.8 11.5 %collective-permute-done.2 = bf16[128,2048]{1,0:T(8,128)(2,1)S(1)} collective-permute-done((bf16[128,2048]{1,0:T(8,128)(2,1)S(1)}, bf16[128,2048]{1,0:T(8,128)(2,1)S(1)}, u32[]{:S(2)}, u32[]{:S(2)}) %collective-permute-start.2) | collective-permute-done | bytes 524320 | tf_op jit(solution)/shard_map/ppermute | solution.py:159
  379.3 2.6 collective-permute-start.9
  382.1 10.6 %collective-permute-done.9 = bf16[64,2048]{1,0:T(8,128)(2,1)S(1)} collective-permute-done((bf16[64,2048]{1,0:T(8,128)(2,1)S(1)}, bf16[64,2048]{1,0:T(8,128)(2,1)S(1)}, u32[]{:S(2)}, u32[]{:S(2)}) %collective-permute-start.9) | collective-permute-done | bytes 262176 | tf_op jit(solution)/shard_map/ppermute | solution.py:159
  392.9 13.5 %collective-permute-done.10 = bf16[64,2048]{1,0:T(8,128)(2,1)S(1)} collective-permute-done((bf16[64,2048]{1,0:T(8,128)(2,1)S(1)}, bf16[64,2048]{1,0:T(8,128)(2,1)S(1)}, u32[]{:S(2)}, u32[]{:S(2)}) %collective-permute-start.10) | collective-permute-done | bytes 262176 | tf_op jit(solution)/shard_map/ppermute | solution.py:163
  409.0 10.3 %collective-permute-done.3 = bf16[64,2048]{1,0:T(8,128)(2,1)S(1)} collective-permute-done((bf16[64,2048]{1,0:T(8,128)(2,1)S(1)}, bf16[64,2048]{1,0:T(8,128)(2,1)S(1)}, u32[]{:S(2)}, u32[]{:S(2)}) %collective-permute-start.3) | collective-permute-done | bytes 262176 | tf_op jit(solution)/shard_map/ppermute | solution.py:159
  419.3 5.8 %collective-permute-done.11 = bf16[128,2048]{1,0:T(8,128)(2,1)S(1)} collective-permute-done((bf16[128,2048]{1,0:T(8,128)(2,1)S(1)}, bf16[128,2048]{1,0:T(8,128)(2,1)S(1)}, u32[]{:S(2)}, u32[]{:S(2)}) %collective-permute-start.11) | collective-permute-done | bytes 524320 | tf_op jit(solution)/shard_map/ppermute | solution.py:163
  426.8 3.4 convert_reduce_fusion.5
  430.2 7.5 %collective-permute-done.4 = bf16[64,2048]{1,0:T(8,128)(2,1)S(1)} collective-permute-done((bf16[64,2048]{1,0:T(8,128)(2,1)S(1)}, bf16[64,2048]{1,0:T(8,128)(2,1)S(1)}, u32[]{:S(2)}, u32[]{:S(2)}) %collective-permute-start.4) | collective-permute-done | bytes 262176 | tf_op jit(solution)/shard_map/ppermute | solution.py:163
  439.5 4.2 fusion.111
  445.4 7.5 %collective-permute-done.5 = bf16[128,2048]{1,0:T(8,128)(2,1)S(1)} collective-permute-done((bf16[128,2048]{1,0:T(8,128)(2,1)S(1)}, bf16[128,2048]{1,0:T(8,128)(2,1)S(1)}, u32[]{:S(2)}, u32[]{:S(2)}) %collective-permute-start.5) | collective-permute-done | bytes 524320 | tf_op jit(solution)/shard_map/ppermute | solution.py:163
  455.1 9.9 %fusion.6 = f32[2048,1536]{0,1:T(8,128)} fusion(bf16[2048,768]{0,1:T(8,128)(2,1)} %collective-permute-done.27, bf16[2048,768]{0,1:T(8,128)(2,1)} %convolution_convert_fusion, pred[]{:T(512)S(6)} %eq.10), kind=kLoop, calls=%fused_computation.11 | loop fusion | flops 31457280 | bytes 18874368 | tf_op jit(solution)/shard_map/convert_element_type | solution.py:194
  465.0 12.6 %copy.195 = f32[2048,1536]{1,0:T(8,128)} copy(f32[2048,1536]{0,1:T(8,128)} %fusion.6) | data formatting | bytes 25165824
  477.6 12.4 %fusion.4 = f32[2048,2048]{0,1:T(8,128)} fusion(bf16[2048,1024]{0,1:T(8,128)(2,1)} %collective-permute-done.30, bf16[2048,1024]{0,1:T(8,128)(2,1)} %fusion.44, pred[]{:T(512)S(6)} %eq.10), kind=kLoop, calls=%fused_computation.7 | loop fusion | flops 41943040 | bytes 25165824 | tf_op jit(solution)/shard_map/convert_element_type | solution.py:194
  489.9 17.6 %copy.196 = f32[2048,2048]{1,0:T(8,128)} copy(f32[2048,2048]{0,1:T(8,128)} %fusion.4) | data formatting | bytes 33554432
  507.5 13.3 %fusion.5 = f32[2048,2048]{0,1:T(8,128)} fusion(bf16[1024,2048]{0,1:T(8,128)(2,1)} %collective-permute-done.32, bf16[1024,2048]{0,1:T(8,128)(2,1)} %fusion.47, pred[]{:T(512)S(6)} %eq.10), kind=kLoop, calls=%fused_computation.9 | loop fusion | flops 41943040 | bytes 25165824 | tf_op jit(solution)/shard_map/convert_element_type | solution.py:194
  520.9 17.7 %copy.197 = f32[2048,2048]{1,0:T(8,128)} copy(f32[2048,2048]{0,1:T(8,128)} %fusion.5) | data formatting | bytes 33554432
  (477 shorter events, 140.3 us)
Async XLA Ops:
  0.6 15.1 %copy-start = (bf16[512,2048]{1,0:T(8,128)(2,1)S(1)}, bf16[512,2048]{1,0:T(8,128)(2,1)}, u32[]{:S(2)}) copy-start(bf16[512,2048]{1,0:T(8,128)(2,1)} %param.17) | copy-start | bytes 6291460
  0.7 11.1 %collective-permute-start.6 = (bf16[256,2048]{1,0:T(8,128)(2,1)}, bf16[256,2048]{1,0:T(8,128)(2,1)S(1)}, u32[]{:S(2)}, u32[]{:S(2)}) collective-permute-start(bf16[256,2048]{1,0:T(8,128)(2,1)} %param.23), channel_id=1, source_target_pairs={{0,4},{4,0},{8,12},{12,8},{16,20},{20,16},{24,28},{28,24},{1,5},{5... | collective-permute-start | bytes 3145736 | tf_op jit(solution)/shard_map/ppermute | solution.py:105
  1.2 32.6 %collective-permute-start.17 = (bf16[256,2048]{1,0:T(8,128)(2,1)}, bf16[256,2048]{1,0:T(8,128)(2,1)}, u32[]{:S(2)}, u32[]{:S(2)}) collective-permute-start(bf16[256,2048]{1,0:T(8,128)(2,1)} %param.12), channel_id=1, source_target_pairs={{0,16},{4,12},{8,24},{12,4},{16,0},{20,28},{24,8},{28,20},{1,17},{... | collective-permute-start | bytes 3145736 | tf_op jit(solution)/shard_map/ppermute | solution.py:102
  3.8 26.5 %collective-permute-start = (bf16[256,2048]{1,0:T(8,128)(2,1)}, bf16[256,2048]{1,0:T(8,128)(2,1)}, u32[]{:S(2)}, u32[]{:S(2)}) collective-permute-start(bf16[256,2048]{1,0:T(8,128)(2,1)} %param.12), channel_id=1, source_target_pairs={{0,4},{4,0},{8,12},{12,8},{16,20},{20,16},{24,28},{28,24},{1,5},{5... | collective-permute-start | bytes 3145736 | tf_op jit(solution)/shard_map/ppermute | solution.py:105
  3.9 26.3 %collective-permute-start.15 = (bf16[256,2048]{1,0:T(8,128)(2,1)}, bf16[256,2048]{1,0:T(8,128)(2,1)}, u32[]{:S(2)}, u32[]{:S(2)}) collective-permute-start(bf16[256,2048]{1,0:T(8,128)(2,1)} %param.12), channel_id=1, source_target_pairs={{0,8},{4,20},{8,0},{12,28},{16,24},{20,4},{24,16},{28,12},{1,9},{5... | collective-permute-start | bytes 3145736 | tf_op jit(solution)/shard_map/ppermute | solution.py:102
  5.3 45.0 %collective-permute-start.21 = (bf16[256,2048]{1,0:T(8,128)(2,1)}, bf16[256,2048]{1,0:T(8,128)(2,1)}, u32[]{:S(2)}, u32[]{:S(2)}) collective-permute-start(bf16[256,2048]{1,0:T(8,128)(2,1)} %param.23), channel_id=1, source_target_pairs={{0,8},{4,20},{8,0},{12,28},{16,24},{20,4},{24,16},{28,12},{1,9},{5... | collective-permute-start | bytes 3145736 | tf_op jit(solution)/shard_map/ppermute | solution.py:102
  8.0 84.8 %copy-start.106 = (f32[768]{0:T(1024)}, f32[768]{0:T(1024)S(1)}, u32[]{:S(2)}) copy-start(f32[768]{0:T(1024)S(1)} %dynamic_slice.19) | copy-start | bytes 9220
  11.8 39.0 %collective-permute-start.23 = (bf16[256,2048]{1,0:T(8,128)(2,1)}, bf16[256,2048]{1,0:T(8,128)(2,1)}, u32[]{:S(2)}, u32[]{:S(2)}) collective-permute-start(bf16[256,2048]{1,0:T(8,128)(2,1)} %param.23), channel_id=1, source_target_pairs={{0,16},{4,12},{8,24},{12,4},{16,0},{20,28},{24,8},{28,20},{1,17},{... | collective-permute-start | bytes 3145736 | tf_op jit(solution)/shard_map/ppermute | solution.py:102
  16.5 13.8 %copy-start.3 = (bf16[256,2048]{1,0:T(8,128)(2,1)S(1)}, bf16[256,2048]{1,0:T(8,128)(2,1)}, u32[]{:S(2)}) copy-start(bf16[256,2048]{1,0:T(8,128)(2,1)} %param.12) | copy-start | bytes 3145732
  30.3 23.4 %collective-permute-start.16 = (bf16[256,2048]{1,0:T(8,128)(2,1)}, bf16[256,2048]{1,0:T(8,128)(2,1)S(1)}, u32[]{:S(2)}, u32[]{:S(2)}) collective-permute-start(bf16[256,2048]{1,0:T(8,128)(2,1)} %collective-permute-done.15), channel_id=1, source_target_pairs={{0,4},{4,0},{8,12},{12,8},{16,20},{20,16},{24,28},{28,24},{1,5},{5... | collective-permute-start | bytes 3145736 | tf_op jit(solution)/shard_map/ppermute | solution.py:105
  33.8 29.0 %copy-start.95 = (f32[512]{0:T(512)}, f32[512]{0:T(512)S(1)}, u32[]{:S(2)}) copy-start(f32[512]{0:T(512)S(1)} %add_rsqrt_fusion.3) | copy-start | bytes 6148
  33.8 101.6 %collective-permute-start.19 = (bf16[256,2048]{1,0:T(8,128)(2,1)}, bf16[256,2048]{1,0:T(8,128)(2,1)}, u32[]{:S(2)}, u32[]{:S(2)}) collective-permute-start(bf16[256,2048]{1,0:T(8,128)(2,1)} %collective-permute-done.17), channel_id=1, source_target_pairs={{0,8},{4,20},{8,0},{12,28},{16,24},{20,4},{24,16},{28,12},{1,9},{5... | collective-permute-start | bytes 3145736 | tf_op jit(solution)/shard_map/ppermute | solution.py:102
  35.2 23.8 %collective-permute-start.18 = (bf16[256,2048]{1,0:T(8,128)(2,1)}, bf16[256,2048]{1,0:T(8,128)(2,1)S(1)}, u32[]{:S(2)}, u32[]{:S(2)}) collective-permute-start(bf16[256,2048]{1,0:T(8,128)(2,1)} %collective-permute-done.17), channel_id=1, source_target_pairs={{0,4},{4,0},{8,12},{12,8},{16,20},{20,16},{24,28},{28,24},{1,5},{5... | collective-permute-start | bytes 3145736 | tf_op jit(solution)/shard_map/ppermute | solution.py:105
  50.3 60.9 %collective-permute-start.22 = (bf16[256,2048]{1,0:T(8,128)(2,1)}, bf16[256,2048]{1,0:T(8,128)(2,1)}, u32[]{:S(2)}, u32[]{:S(2)}) collective-permute-start(bf16[256,2048]{1,0:T(8,128)(2,1)} %collective-permute-done.21), channel_id=1, source_target_pairs={{0,4},{4,0},{8,12},{12,8},{16,20},{20,16},{24,28},{28,24},{1,5},{5... | collective-permute-start | bytes 3145736 | tf_op jit(solution)/shard_map/ppermute | solution.py:105
  50.7 97.3 %collective-permute-start.24 = (bf16[256,2048]{1,0:T(8,128)(2,1)}, bf16[256,2048]{1,0:T(8,128)(2,1)}, u32[]{:S(2)}, u32[]{:S(2)}) collective-permute-start(bf16[256,2048]{1,0:T(8,128)(2,1)} %collective-permute-done.23), channel_id=1, source_target_pairs={{0,4},{4,0},{8,12},{12,8},{16,20},{20,16},{24,28},{28,24},{1,5},{5... | collective-permute-start | bytes 3145736 | tf_op jit(solution)/shard_map/ppermute | solution.py:105
  53.6 120.0 %collective-permute-start.25 = (bf16[256,2048]{1,0:T(8,128)(2,1)}, bf16[256,2048]{1,0:T(8,128)(2,1)}, u32[]{:S(2)}, u32[]{:S(2)}) collective-permute-start(bf16[256,2048]{1,0:T(8,128)(2,1)} %collective-permute-done.23), channel_id=1, source_target_pairs={{0,8},{4,20},{8,0},{12,28},{16,24},{20,4},{24,16},{28,12},{1,9},{5... | collective-permute-start | bytes 3145736 | tf_op jit(solution)/shard_map/ppermute | solution.py:102
  60.7 11.5 %slice-start.8 = ((s8[6291456]{0:T(1024)(128)(4,1)}), s8[4194304]{0:T(1024)(128)(4,1)S(1)}, s32[]{:S(2)}) async-start(s8[6291456]{0:T(1024)(128)(4,1)} %bitcast.204), calls=%async_computation.8 | async-start | bytes 8388608
  62.8 9.4 %slice-start.9 = ((s8[6291456]{0:T(1024)(128)(4,1)}), s8[2097152]{0:T(1024)(128)(4,1)S(1)}, s32[]{:S(2)}) async-start(s8[6291456]{0:T(1024)(128)(4,1)} %bitcast.204), calls=%async_computation.9 | async-start | bytes 4194304
  116.2 11.2 %copy-start.15 = (bf16[2,256,4,64]{1,3,2,0:T(8,128)(2,1)}, bf16[2,256,4,64]{1,3,2,0:T(8,128)(2,1)S(1)}, u32[]{:S(2)}) copy-start(bf16[2,256,4,64]{1,3,2,0:T(8,128)(2,1)S(1)} %copy.153) | copy-start | bytes 786436
  129.3 9.7 %slice-start.19 = ((s8[8388608]{0:T(1024)(128)(4,1)}), s8[4194304]{0:T(1024)(128)(4,1)S(1)}, s32[]{:S(2)}) async-start(s8[8388608]{0:T(1024)(128)(4,1)} %bitcast.238), calls=%async_computation.19 | async-start | bytes 8388608
  130.6 8.4 %slice-start.20 = ((s8[8388608]{0:T(1024)(128)(4,1)}), s8[4194304]{0:T(1024)(128)(4,1)S(1)}, s32[]{:S(2)}) async-start(s8[8388608]{0:T(1024)(128)(4,1)} %bitcast.238), calls=%async_computation.20 | async-start | bytes 8388608
  135.3 7.8 %copy-start.108 = (f32[512,1024]{1,0:T(8,128)}, f32[512,1024]{1,0:T(8,128)S(1)}, u32[]{:S(2)}) copy-start(f32[512,1024]{1,0:T(8,128)S(1)} %fusion.78) | copy-start | bytes 6291460
  135.4 48.9 %collective-permute-start.20 = (bf16[256,2048]{1,0:T(8,128)(2,1)}, bf16[256,2048]{1,0:T(8,128)(2,1)S(1)}, u32[]{:S(2)}, u32[]{:S(2)}) collective-permute-start(bf16[256,2048]{1,0:T(8,128)(2,1)} %collective-permute-done.19), channel_id=1, source_target_pairs={{0,4},{4,0},{8,12},{12,8},{16,20},{20,16},{24,28},{28,24},{1,5},{5... | collective-permute-start | bytes 3145736 | tf_op jit(solution)/shard_map/ppermute | solution.py:105
  135.7 7.4 %slice-start.15 = ((s8[8388608]{0:T(1024)(128)(4,1)}), s8[4194304]{0:T(1024)(128)(4,1)S(1)}, s32[]{:S(2)}) async-start(s8[8388608]{0:T(1024)(128)(4,1)} %bitcast.234), calls=%async_computation.15 | async-start | bytes 8388608
  173.7 60.0 %collective-permute-start.26 = (bf16[256,2048]{1,0:T(8,128)(2,1)}, bf16[256,2048]{1,0:T(8,128)(2,1)}, u32[]{:S(2)}, u32[]{:S(2)}) collective-permute-start(bf16[256,2048]{1,0:T(8,128)(2,1)} %collective-permute-done.25), channel_id=1, source_target_pairs={{0,4},{4,0},{8,12},{12,8},{16,20},{20,16},{24,28},{28,24},{1,5},{5... | collective-permute-start | bytes 3145736 | tf_op jit(solution)/shard_map/ppermute | solution.py:105
  173.9 17.4 %slice-start.10 = ((s8[6291456]{0:T(1024)(128)(4,1)}), s8[4194304]{0:T(1024)(128)(4,1)S(1)}, s32[]{:S(2)}) async-start(s8[6291456]{0:T(1024)(128)(4,1)} %bitcast.206), calls=%async_computation.10 | async-start | bytes 8388608
  176.9 14.4 %slice-start.11 = ((s8[6291456]{0:T(1024)(128)(4,1)}), s8[2097152]{0:T(1024)(128)(4,1)S(1)}, s32[]{:S(2)}) async-start(s8[6291456]{0:T(1024)(128)(4,1)} %bitcast.206), calls=%async_computation.11 | async-start | bytes 4194304
  246.7 12.8 %slice-start.17 = ((s8[8388608]{0:T(1024)(128)(4,1)}), s8[4194304]{0:T(1024)(128)(4,1)S(1)}, s32[]{:S(2)}) async-start(s8[8388608]{0:T(1024)(128)(4,1)} %bitcast.236), calls=%async_computation.17 | async-start | bytes 8388608
  267.8 7.1 %copy-start.115 = (bf16[512,1024]{1,0:T(8,128)(2,1)}, bf16[512,1024]{1,0:T(8,128)(2,1)S(1)}, u32[]{:S(2)}) copy-start(bf16[512,1024]{1,0:T(8,128)(2,1)S(1)} %get-tuple-element.150) | copy-start | bytes 3145732
  267.8 15.5 %slice-start.12 = ((s8[6291456]{0:T(1024)(128)(4,1)}), s8[4194304]{0:T(1024)(128)(4,1)S(1)}, s32[]{:S(2)}) async-start(s8[6291456]{0:T(1024)(128)(4,1)} %bitcast.208), calls=%async_computation.12 | async-start | bytes 8388608
  274.9 8.4 %slice-start.13 = ((s8[6291456]{0:T(1024)(128)(4,1)}), s8[2097152]{0:T(1024)(128)(4,1)S(1)}, s32[]{:S(2)}) async-start(s8[6291456]{0:T(1024)(128)(4,1)} %bitcast.208), calls=%async_computation.13 | async-start | bytes 4194304
  281.9 69.8 %collective-permute-start.1 = (bf16[256,2048]{1,0:T(8,128)(2,1)}, bf16[256,2048]{1,0:T(8,128)(2,1)}, u32[]{:S(2)}, u32[]{:S(2)}) collective-permute-start(bf16[256,2048]{1,0:T(8,128)(2,1)} %slice.502), channel_id=1, source_target_pairs={{0,4},{4,0},{8,12},{12,8},{16,20},{20,16},{24,28},{28,24},{1,5},{5... | collective-permute-start | bytes 3145736 | tf_op jit(solution)/shard_map/ppermute | solution.py:105
  287.9 61.8 %collective-permute-start.7 = (bf16[256,2048]{1,0:T(8,128)(2,1)}, bf16[256,2048]{1,0:T(8,128)(2,1)}, u32[]{:S(2)}, u32[]{:S(2)}) collective-permute-start(bf16[256,2048]{1,0:T(8,128)(2,1)} %slice.501), channel_id=1, source_target_pairs={{0,4},{4,0},{8,12},{12,8},{16,20},{20,16},{24,28},{28,24},{1,5},{5... | collective-permute-start | bytes 3145736 | tf_op jit(solution)/shard_map/ppermute | solution.py:105
  292.4 9.0 %copy-start.50 = (bf16[2,256,4,64]{1,3,2,0:T(8,128)(2,1)S(1)}, bf16[2,256,4,64]{1,3,2,0:T(8,128)(2,1)}, u32[]{:S(2)}) copy-start(bf16[2,256,4,64]{1,3,2,0:T(8,128)(2,1)} %get-tuple-element.171) | copy-start | bytes 786436
  292.4 9.3 %copy-start.48 = (bf16[2,256,4,64]{1,3,2,0:T(8,128)(2,1)S(1)}, bf16[2,256,4,64]{1,3,2,0:T(8,128)(2,1)}, u32[]{:S(2)}) copy-start(bf16[2,256,4,64]{1,3,2,0:T(8,128)(2,1)} %get-tuple-element.167) | copy-start | bytes 786436
  300.8 154.3 %collective-permute-start.27 = (bf16[2048,768]{0,1:T(8,128)(2,1)}, bf16[2048,768]{0,1:T(8,128)(2,1)}, u32[]{:S(2)}, u32[]{:S(2)}) collective-permute-start(bf16[2048,768]{0,1:T(8,128)(2,1)} %convolution_convert_fusion), channel_id=1, source_target_pairs={{0,4},{4,0},{8,12},{12,8},{16,20},{20,16},{24,28},{28,24},{1,5},{5... | collective-permute-start | bytes 9437192 | tf_op jit(solution)/shard_map/ppermute | solution.py:105
  301.1 47.6 %collective-permute-start.28 = (f32[768]{0:T(1024)S(1)}, f32[768]{0:T(1024)S(1)}, u32[]{:S(2)}, u32[]{:S(2)}) collective-permute-start(f32[768]{0:T(1024)S(1)} %add.369), channel_id=1, source_target_pairs={{0,4},{4,0},{8,12},{12,8},{16,20},{20,16},{24,28},{28,24},{1,5},{5... | collective-permute-start | bytes 9224 | tf_op jit(solution)/shard_map/ppermute | solution.py:105
  302.1 6.1 %copy-start.66 = (bf16[512,2048]{1,0:T(8,128)(2,1)S(1)}, bf16[512,2048]{1,0:T(8,128)(2,1)}, u32[]{:S(2)}) copy-start(bf16[512,2048]{1,0:T(8,128)(2,1)} %copy-done.65) | copy-start | bytes 6291460
  302.1 6.1 %copy-start.113 = (f32[512,1024]{1,0:T(8,128)S(1)}, f32[512,1024]{1,0:T(8,128)}, u32[]{:S(2)}) copy-start(f32[512,1024]{1,0:T(8,128)} %get-tuple-element.154) | copy-start | bytes 6291460
  308.0 131.0 %collective-permute-start.29 = (bf16[256,2048]{1,0:T(8,128)(2,1)S(1)}, bf16[256,2048]{1,0:T(8,128)(2,1)}, u32[]{:S(2)}, u32[]{:S(2)}) collective-permute-start(bf16[256,2048]{1,0:T(8,128)(2,1)S(1)} %convolution_convert_fusion.1), channel_id=1, source_target_pairs={{0,4},{4,0},{8,12},{12,8},{16,20},{20,16},{24,28},{28,24},{1,5},{5... | collective-permute-start | bytes 3145736 | tf_op jit(solution)/shard_map/ppermute | solution.py:105
  308.2 6.8 %copy-start.21 = (bf16[512,2048]{1,0:T(8,128)(2,1)S(1)}, bf16[512,2048]{1,0:T(8,128)(2,1)}, u32[]{:S(2)}) copy-start(bf16[512,2048]{1,0:T(8,128)(2,1)} %copy-done.18) | copy-start | bytes 6291460
  343.8 6.2 %copy-start.8 = (f32[512,2048]{1,0:T(8,128)S(1)}, f32[512,2048]{1,0:T(8,128)}, u32[]{:S(2)}) copy-start(f32[512,2048]{1,0:T(8,128)} %copy-done.7) | copy-start | bytes 12582916
  348.7 190.0 %copy-start.94 = (f32[2048]{0:T(1024)}, f32[2048]{0:T(1024)S(1)}, u32[]{:S(2)}) copy-start(f32[2048]{0:T(1024)S(1)} %convert_reduce_fusion) | copy-start | bytes 24580
  348.7 128.8 %collective-permute-start.30 = (bf16[2048,1024]{0,1:T(8,128)(2,1)}, bf16[2048,1024]{0,1:T(8,128)(2,1)}, u32[]{:S(2)}, u32[]{:S(2)}) collective-permute-start(bf16[2048,1024]{0,1:T(8,128)(2,1)} %fusion.44), channel_id=1, source_target_pairs={{0,4},{4,0},{8,12},{12,8},{16,20},{20,16},{24,28},{28,24},{1,5},{5... | collective-permute-start | bytes 12582920 | tf_op jit(solution)/shard_map/ppermute | solution.py:105
  349.7 56.8 %collective-permute-start.31 = (f32[1024]{0:T(1024)S(1)}, f32[1024]{0:T(1024)S(1)}, u32[]{:S(2)}, u32[]{:S(2)}) collective-permute-start(f32[1024]{0:T(1024)S(1)} %add_add_fusion.1), channel_id=1, source_target_pairs={{0,4},{4,0},{8,12},{12,8},{16,20},{20,16},{24,28},{28,24},{1,5},{5... | collective-permute-start | bytes 12296 | tf_op jit(solution)/shard_map/ppermute | solution.py:105
  351.7 14.3 %collective-permute-start.8 = (bf16[128,2048]{1,0:T(8,128)(2,1)S(1)}, bf16[128,2048]{1,0:T(8,128)(2,1)S(1)}, u32[]{:S(2)}, u32[]{:S(2)}) collective-permute-start(bf16[128,2048]{1,0:T(8,128)(2,1)S(1)} %broadcast_select_fusion), channel_id=1, source_target_pairs={{0,1},{1,0},{2,3},{3,2},{4,5},{5,4},{6,7},{7,6},{8,9},{9,8},{10,11... | collective-permute-start | bytes 1572872 | tf_op jit(solution)/shard_map/ppermute | solution.py:159
  366.0 13.3 %collective-permute-start.2 = (bf16[128,2048]{1,0:T(8,128)(2,1)S(1)}, bf16[128,2048]{1,0:T(8,128)(2,1)S(1)}, u32[]{:S(2)}, u32[]{:S(2)}) collective-permute-start(bf16[128,2048]{1,0:T(8,128)(2,1)S(1)} %broadcast_select_fusion.1), channel_id=1, source_target_pairs={{0,1},{1,0},{2,3},{3,2},{4,5},{5,4},{6,7},{7,6},{8,9},{9,8},{10,11... | collective-permute-start | bytes 1572872 | tf_op jit(solution)/shard_map/ppermute | solution.py:159
  379.3 13.4 %collective-permute-start.9 = (bf16[64,2048]{1,0:T(8,128)(2,1)S(1)}, bf16[64,2048]{1,0:T(8,128)(2,1)S(1)}, u32[]{:S(2)}, u32[]{:S(2)}) collective-permute-start(bf16[64,2048]{1,0:T(8,128)(2,1)S(1)} %broadcast_select_fusion.2), channel_id=1, source_target_pairs={{0,2},{1,3},{2,0},{3,1},{4,6},{5,7},{6,4},{7,5},{8,10},{9,11},{10,... | collective-permute-start | bytes 786440 | tf_op jit(solution)/shard_map/ppermute | solution.py:159
  381.9 44.1 %copy-start.2 = (f32[512,2048]{1,0:T(8,128)S(1)}, f32[512,2048]{1,0:T(8,128)}, u32[]{:S(2)}) copy-start(f32[512,2048]{1,0:T(8,128)} %get-tuple-element.51) | copy-start | bytes 12582916
  382.1 43.8 %copy-start.91 = (f32[2048]{0:T(1024)S(1)}, f32[2048]{0:T(1024)}, u32[]{:S(2)}) copy-start(f32[2048]{0:T(1024)} %param.13) | copy-start | bytes 24580
  392.8 13.6 %collective-permute-start.10 = (bf16[64,2048]{1,0:T(8,128)(2,1)S(1)}, bf16[64,2048]{1,0:T(8,128)(2,1)S(1)}, u32[]{:S(2)}, u32[]{:S(2)}) collective-permute-start(bf16[64,2048]{1,0:T(8,128)(2,1)S(1)} %add_convert_fusion.4), channel_id=1, source_target_pairs={{0,2},{1,3},{2,0},{3,1},{4,6},{5,7},{6,4},{7,5},{8,10},{9,11},{10,... | collective-permute-start | bytes 786440 | tf_op jit(solution)/shard_map/ppermute | solution.py:163
  406.4 12.8 %collective-permute-start.3 = (bf16[64,2048]{1,0:T(8,128)(2,1)S(1)}, bf16[64,2048]{1,0:T(8,128)(2,1)S(1)}, u32[]{:S(2)}, u32[]{:S(2)}) collective-permute-start(bf16[64,2048]{1,0:T(8,128)(2,1)S(1)} %broadcast_select_fusion.3), channel_id=1, source_target_pairs={{0,2},{1,3},{2,0},{3,1},{4,6},{5,7},{6,4},{7,5},{8,10},{9,11},{10,... | collective-permute-start | bytes 786440 | tf_op jit(solution)/shard_map/ppermute | solution.py:159
  406.5 18.6 %collective-permute-start.11 = (bf16[128,2048]{1,0:T(8,128)(2,1)S(1)}, bf16[128,2048]{1,0:T(8,128)(2,1)S(1)}, u32[]{:S(2)}, u32[]{:S(2)}) collective-permute-start(bf16[128,2048]{1,0:T(8,128)(2,1)S(1)} %maximum_select_fusion.7), channel_id=1, source_target_pairs={{0,1},{1,0},{2,3},{3,2},{4,5},{5,4},{6,7},{7,6},{8,9},{9,8},{10,11... | collective-permute-start | bytes 1572872 | tf_op jit(solution)/shard_map/ppermute | solution.py:163
  409.0 17.8 %slice-start.14 = ((f32[512]{0:T(512)}), f32[256]{0:T(256)S(1)}, s32[]{:S(2)}) async-start(f32[512]{0:T(512)} %copy-done.95), calls=%async_computation.14 | async-start | bytes 2048 | tf_op jit(solution)/shard_map/slice | solution.py:141
  419.2 88.3 %collective-permute-start.32 = (bf16[1024,2048]{0,1:T(8,128)(2,1)}, bf16[1024,2048]{0,1:T(8,128)(2,1)}, u32[]{:S(2)}, u32[]{:S(2)}) collective-permute-start(bf16[1024,2048]{0,1:T(8,128)(2,1)} %fusion.47), channel_id=1, source_target_pairs={{0,4},{4,0},{8,12},{12,8},{16,20},{20,16},{24,28},{28,24},{1,5},{5... | collective-permute-start | bytes 12582920 | tf_op jit(solution)/shard_map/ppermute | solution.py:105
  425.1 12.6 %collective-permute-start.4 = (bf16[64,2048]{1,0:T(8,128)(2,1)S(1)}, bf16[64,2048]{1,0:T(8,128)(2,1)S(1)}, u32[]{:S(2)}, u32[]{:S(2)}) collective-permute-start(bf16[64,2048]{1,0:T(8,128)(2,1)S(1)} %add_convert_fusion.5), channel_id=1, source_target_pairs={{0,2},{1,3},{2,0},{3,1},{4,6},{5,7},{6,4},{7,5},{8,10},{9,11},{10,... | collective-permute-start | bytes 786440 | tf_op jit(solution)/shard_map/ppermute | solution.py:163
  437.7 1.2 collective-permute-start.12
  438.9 14.0 %collective-permute-start.5 = (bf16[128,2048]{1,0:T(8,128)(2,1)S(1)}, bf16[128,2048]{1,0:T(8,128)(2,1)S(1)}, u32[]{:S(2)}, u32[]{:S(2)}) collective-permute-start(bf16[128,2048]{1,0:T(8,128)(2,1)S(1)} %maximum_select_fusion.6), channel_id=1, source_target_pairs={{0,1},{1,0},{2,3},{3,2},{4,5},{5,4},{6,7},{7,6},{8,9},{9,8},{10,11... | collective-permute-start | bytes 1572872 | tf_op jit(solution)/shard_map/ppermute | solution.py:163
  438.9 14.0 %copy-start.4 = (bf16[256,2048]{1,0:T(8,128)(2,1)S(1)}, bf16[256,2048]{1,0:T(8,128)(2,1)}, u32[]{:S(2)}) copy-start(bf16[256,2048]{1,0:T(8,128)(2,1)} %param.12) | copy-start | bytes 3145732
  439.0 14.0 %copy-start.96 = (f32[2048]{0:T(1024)S(1)}, f32[2048]{0:T(1024)}, u32[]{:S(2)}) copy-start(f32[2048]{0:T(1024)} %param.22) | copy-start | bytes 24580
  439.0 13.9 %copy-start.97 = (f32[2048]{0:T(1024)S(1)}, f32[2048]{0:T(1024)}, u32[]{:S(2)}) copy-start(f32[2048]{0:T(1024)} %param.18) | copy-start | bytes 24580
  439.0 4.7 collective-permute-start.13
  443.8 10.7 %collective-permute-start.14 = (f32[2,2048]{1,0:T(2,128)S(1)}, f32[2,2048]{1,0:T(2,128)S(1)}, u32[]{:S(2)}, u32[]{:S(2)}) collective-permute-start(f32[2,2048]{1,0:T(2,128)S(1)} %fusion.298), channel_id=1, source_target_pairs={{0,16},{4,20},{8,24},{12,28},{16,0},{20,4},{24,8},{28,12},{1,17},{... | collective-permute-start | bytes 49160 | tf_op jit(solution)/shard_map/ppermute | solution.py:181
  520.9 18.4 %copy-start.1 = (bf16[512,2048]{1,0:T(8,128)(2,1)S(1)}, bf16[512,2048]{1,0:T(8,128)(2,1)}, u32[]{:S(2)}) copy-start(bf16[512,2048]{1,0:T(8,128)(2,1)} %param.17) | copy-start | bytes 6291460
  (106 other events, 262.8 us)
